TPU v7x, 32 devices: a whole 2x2x4 slice. The times are simulated.
32 devices in a mesh: gx: 4 (over z), gy: 2 (over x), gz: 4 (over y, core).
Axes of the slice: x: 2, y: 2, z: 4, core: 2. Of those that a mesh axis runs over, the one named last changes fastest.
Arguments:
- amplitudes: float32 [2, 8388608], P(None, ('gx', 'gy', 'gz')), may hold values from -6 to 6
- couplings: float32 [23], replicated, may hold values from -1.2 to 1.2
- fields: float32 [23], replicated, may hold values from 0.3 to 1.2
Outputs:
- evolved: float32 [2, 8388608], P(None, ('gx', 'gy', 'gz'))
All inputs are finite; a program needn't handle non-finite values.
Results may differ from a plain program's by a relative error of at most 0.000098.
Values sent between devices are 32-bit elements; how exact they have to be, the bound alone decides.
A program may use at most 64 MiB of HBM per device.

v0:
```python
import functools
import math

import jax
import jax.numpy as jnp
from jax import lax
from jax.experimental import pallas as pl
from jax.experimental.pallas import tpu as pltpu
from jax.sharding import PartitionSpec as P

MESH = pl.DeviceIdType.MESH
AXES = ("gx", "gy", "gz")
LANES = 128
CHUNK_BITS = 3
LOW_BITS = 5
VMEM = 67043328
EXACT = lax.Precision.HIGHEST


def log2(size):
    return size.bit_length() - 1


def bits_set(value, first, last):
    total = jnp.zeros_like(value)
    for bit in range(first, last):
        total = total + ((value >> bit) & 1)
    return total


def swapped(value):
    rows = value.shape[0]
    even = lax.broadcasted_iota(jnp.int32, value.shape, 0) & 1 == 0
    return jnp.where(even, pltpu.roll(value, rows - 1, 0), pltpu.roll(value, 1, 0))


def kernel(sizes, qubits, couplings, fields, amp, done, held, state, landed, low_c, low_s, high_c, high_s, cosine, sine, rows_w, lanes_w, in_sem, send_sem, recv_sem):
    rows_all = held.shape[0]
    chunks = 1 << CHUNK_BITS
    chunk = rows_all // chunks
    lane_bits = log2(LANES)
    local_bits = log2(rows_all // 2) + lane_bits
    chunk_low = local_bits - CHUNK_BITS
    low_top = lane_bits + LOW_BITS
    tile = 2 << LOW_BITS
    highs = rows_all // tile
    place = {axis: lax.axis_index(axis) for axis in AXES}
    device = jnp.int32(0)
    for axis in AXES:
        device = device * sizes[axis] + place[axis]

    stages = {axis: [] for axis in AXES}
    qubit = local_bits
    for axis in reversed(AXES):
        for bit in range(log2(sizes[axis])):
            stages[axis].append((axis, bit, qubit))
            qubit += 1
    far = list(reversed(stages["gx"]))
    near = stages["gy"] + list(reversed(stages["gz"]))
    turn = near[1::-1] + near[2:]
    half = (len(far) + 1) // 2
    plans = (far[:half] + near + far[half:], far[half:] + turn + far[:half])
    count = len(plans[0])

    def partner(axis, bit):
        return tuple(place[a] ^ (1 << bit) if a == axis else place[a] for a in AXES)

    loads = [pltpu.make_async_copy(amp.at[pl.ds(c * chunk, chunk)], held.at[pl.ds(c * chunk, chunk)], in_sem.at[c]) for c in range(chunks)]
    for load in loads:
        load.start()
    barrier = pltpu.get_barrier_semaphore()
    for axis, bit, _ in plans[0]:
        pl.semaphore_signal(barrier, inc=1, device_id=partner(axis, bit), device_id_type=MESH)

    for q in range(qubits):
        cosine[pl.ds(q, 1), :] = jnp.full((1, LANES), fields[q], jnp.float32)
    angles = cosine[...]
    cosine[...] = jnp.cos(angles)
    sine[...] = jnp.sin(angles)

    def angle_of(position, bonds):
        total = jnp.zeros(position.shape, jnp.float32)
        for q in bonds:
            parity = (position >> q ^ position >> ((q + 1) % qubits)) & 1
            total = total + couplings[q] * (1.0 - 2.0 * parity.astype(jnp.float32))
        return total

    row = lax.broadcasted_iota(jnp.int32, (2 * tile, LANES), 0)
    lane = lax.broadcasted_iota(jnp.int32, (2 * tile, LANES), 1)
    position = (device << local_bits) + ((row >> 1) << lane_bits) + lane
    turns = bits_set(position, 0, low_top) & 3
    low = angle_of(position, list(range(low_top)) + [qubits - 1]) + turns.astype(jnp.float32) * (math.pi / 2)
    low_c[...] = jnp.cos(low)
    low_s[...] = jnp.sin(low)
    high_row = lax.broadcasted_iota(jnp.int32, (highs, LANES), 0)
    position = (device << local_bits) + (high_row << low_top)
    turns = bits_set(position, low_top, qubits) & 3
    high = angle_of(position, range(low_top, qubits - 1)) + turns.astype(jnp.float32) * (math.pi / 2)
    high_c[...] = jnp.cos(high)
    high_s[...] = jnp.sin(high)

    for load in loads:
        load.wait()

    @pl.loop(0, chunk // 8)
    def _(step):
        sign = jnp.where(lax.broadcasted_iota(jnp.int32, (8, LANES), 0) & 1 == 0, 1.0, -1.0)
        at = pl.multiple_of(step * 8, 8)
        low_at = pl.multiple_of(lax.rem(step * 8, 2 * tile), 8)
        c_low = low_c[pl.ds(low_at, 8), :]
        s_low = low_s[pl.ds(low_at, 8), :]
        high_at = step * 8 // tile
        parts = []
        for c in range(chunks):
            number = c * (chunk // tile) + high_at
            c_high = high_c[pl.ds(number, 1), :]
            s_high = high_s[pl.ds(number, 1), :]
            value = held[pl.ds(pl.multiple_of(c * chunk + at, 8), 8), :]
            c_all = c_low * c_high - s_low * s_high
            s_all = s_low * c_high + c_low * s_high
            parts.append(value * c_all + swapped(value) * (s_all * sign))
        for bit in range(CHUNK_BITS):
            c_q = cosine[pl.ds(chunk_low + bit, 1), :]
            s_q = sine[pl.ds(chunk_low + bit, 1), :]
            mixed = list(parts)
            for c in range(chunks):
                if not c >> bit & 1:
                    first, second = parts[c], parts[c | 1 << bit]
                    mixed[c] = c_q * first + s_q * second
                    mixed[c | 1 << bit] = s_q * first - c_q * second
            parts = mixed
        for c in range(chunks):
            state[0, pl.ds(pl.multiple_of(c * chunk + at, 8), 8), :] = parts[c]

    def send(c, k):
        axis, bit, _ = plans[c % 2][k]
        span = pl.ds(c * chunk, chunk)
        return pltpu.make_async_remote_copy(
            src_ref=state.at[k, span],
            dst_ref=landed.at[k, span],
            send_sem=send_sem.at[k, c],
            recv_sem=recv_sem.at[k, c],
            device_id=partner(axis, bit),
            device_id_type=MESH,
        )

    pl.semaphore_wait(barrier, count)
    for c in range(chunks):
        send(c, 0).start()

    def matrix(shape, first_row, skip, first, last):
        there = lax.broadcasted_iota(jnp.int32, shape, 0) + first_row
        here = lax.broadcasted_iota(jnp.int32, shape, 1)
        total = jnp.ones(shape, jnp.float32)
        if skip:
            total = jnp.where((there ^ here) & ((1 << skip) - 1) == 0, total, 0.0)
        repeat = shape[1] // LANES
        for q in range(first, last):
            bit = q - first + skip
            c_q = jnp.concatenate([cosine[pl.ds(q, 1), :]] * repeat, axis=1)
            s_q = jnp.concatenate([sine[pl.ds(q, 1), :]] * repeat, axis=1)
            up, left = there >> bit & 1, here >> bit & 1
            total = total * jnp.where(up ^ left == 1, s_q, jnp.where(up == 1, -c_q, c_q))
        return total

    lanes_w[...] = matrix((LANES, LANES), 0, 0, 0, lane_bits)

    @pl.loop(0, chunk // 8)
    def _(step):
        at = pl.multiple_of(step * 8, 8)
        rows_w[pl.ds(at, 8), :] = matrix((8, chunk), at, 1, lane_bits, chunk_low)

    block = LANES

    def local(c, source, target):
        @pl.loop(0, chunk // block)
        def _(step):
            at = pl.multiple_of(c * chunk + step * block, block)
            source[pl.ds(at, block), :] = jnp.dot(source[pl.ds(at, block), :], lanes_w[...], precision=EXACT, preferred_element_type=jnp.float32)

        @pl.loop(0, chunk // block)
        def _(step):
            at = pl.multiple_of(step * block, block)
            target[pl.ds(pl.multiple_of(c * chunk + at, block), block), :] = jnp.dot(
                rows_w[pl.ds(at, block), :], source[pl.ds(c * chunk, chunk), :], precision=EXACT, preferred_element_type=jnp.float32
            )

    def combine(c, k, target, last):
        axis, bit, q = plans[c % 2][k]
        own = 1.0 - 2.0 * ((place[axis] >> bit) & 1).astype(jnp.float32)

        @pl.loop(0, chunk // tile)
        def _(step):
            at = pl.multiple_of(c * chunk + step * tile, tile)
            c_q = cosine[pl.ds(q, 1), :] * own
            s_q = sine[pl.ds(q, 1), :]
            value = c_q * state[k, pl.ds(at, tile), :] + s_q * landed[k, pl.ds(at, tile), :]
            if last:
                row = lax.broadcasted_iota(jnp.int32, (tile, LANES), 0)
                lane = lax.broadcasted_iota(jnp.int32, (tile, LANES), 1)
                inner = ((row >> 1) << lane_bits) + lane
                number = (device << local_bits) + ((c * (chunk // tile) + step) << low_top)
                turns = bits_set(inner, 0, low_top) + bits_set(number, low_top, qubits)
                value = jnp.where(turns & 1 == 1, swapped(value), value)
                value = jnp.where((turns + (row & 1)) & 2 == 2, -value, value)
            target[pl.ds(at, tile), :] = value

    events = [(c // 2 + 0.5 * k if k < count - 1 else 2 * chunks + c // 2, k, c) for c in range(chunks) for k in range(count)]
    for _, k, c in sorted(events):
        send(c, k).wait_recv()
        if k == count - 1:
            combine(c, k, done, True)
        elif k == 0:
            combine(c, k, done, False)
            local(c, done, state.at[1])
            send(c, 1).start()
        else:
            combine(c, k, state.at[k + 1], False)
            send(c, k + 1).start()
    for k in range(count):
        for c in range(chunks):
            send(c, k).wait_send()


def solution(mesh):
    sizes = {axis: mesh.shape[axis] for axis in AXES}
    count = sum(log2(size) for size in sizes.values())

    def step(amplitudes, couplings, fields):
        local = amplitudes.shape[1]
        qubits = couplings.shape[0]
        rows = 2 * local // LANES
        chunks = 1 << CHUNK_BITS
        chunk = rows // chunks
        tile = 2 << LOW_BITS
        table = -(-qubits // 8) * 8
        woven = amplitudes.reshape(2, local // LANES, LANES).transpose(1, 0, 2).reshape(rows, LANES)
        vmem = lambda *shape: pltpu.VMEM(shape, jnp.float32)
        result = pl.pallas_call(
            functools.partial(kernel, sizes, qubits),
            out_shape=pltpu.VMEM((rows, LANES), jnp.float32),
            in_specs=[pl.BlockSpec(memory_space=pltpu.SMEM)] * 2 + [pl.BlockSpec(memory_space=pltpu.HBM)],
            out_specs=pl.BlockSpec(memory_space=pltpu.VMEM),
            scratch_shapes=[
                vmem(rows, LANES),
                vmem(count, rows, LANES),
                vmem(count, rows, LANES),
                vmem(2 * tile, LANES),
                vmem(2 * tile, LANES),
                vmem(rows // tile, LANES),
                vmem(rows // tile, LANES),
                vmem(table, LANES),
                vmem(table, LANES),
                vmem(chunk, chunk),
                vmem(LANES, LANES),
                pltpu.SemaphoreType.DMA((chunks,)),
                pltpu.SemaphoreType.DMA((count, chunks)),
                pltpu.SemaphoreType.DMA((count, chunks)),
            ],
            compiler_params=pltpu.CompilerParams(
                collective_id=0, has_side_effects=True, vmem_limit_bytes=VMEM - 4 * rows * LANES
            ),
        )(couplings, fields, woven)
        return result.reshape(local // LANES, 2, LANES).transpose(1, 0, 2).reshape(2, local)

    placed = (P(None, AXES), P(), P())
    return jax.shard_map(step, mesh=mesh, in_specs=placed, out_specs=P(None, AXES), check_vma=False)
```

profile of v0, /device:TPU:9, one launch (start us, length us, event | category | flops | bytes accessed | tf_op | source)
XLA Modules:
  0.0 99.5 jit_solution(17943519344569394253)
XLA Ops:
  0.0 98.1 %shard_map.37 = f32[4096,128]{1,0:T(8,128)S(1)} custom-call(f32[23]{0:T(128)} %couplings.1, f32[23]{0:T(128)} %fields.1, f32[4096,128]{1,0:T(8,128)} %bitcast.11), custom_call_target="tpu_custom_call" | custom-call | tf_op jit(solution)/shard_map/pallas_call | solution.py:239
  98.1 1.3 %copy.7 = f32[2,262144]{1,0:T(2,128)} copy(f32[2,262144]{1,0:T(2,128)S(1)} %bitcast.10) | data formatting | bytes 4194304
where the time goes:
time: 101 us; the launch traced here: 99.5 us
  Pallas kernels  98.1 us (97%)
  local copies, waits for them, and re-layouts  1.32 us (1%)
    pallas_call x1, Pallas kernels, step(): pl.pallas_call(functools.partial(kernel, sizes, qubits), out_shape=pltpu....  98.1 us

commit v1 on v0

v1 whole, which is shorter than its diff:
```python
import functools
import math

import jax
import jax.numpy as jnp
from jax import lax
from jax.experimental import pallas as pl
from jax.experimental.pallas import tpu as pltpu
from jax.sharding import PartitionSpec as P

MESH = pl.DeviceIdType.MESH
AXES = ("gx", "gy", "gz")
LANES = 128
CHUNK_BITS = 3
TAIL_PARTS = 8
AHEAD = 3
VMEM = 67043328
EXACT = lax.Precision.HIGHEST


def log2(size):
    return size.bit_length() - 1


def bits_set(value, first, last):
    total = jnp.zeros_like(value)
    for bit in range(first, last):
        total = total + ((value >> bit) & 1)
    return total


def swapped(value):
    rows = value.shape[0]
    even = lax.broadcasted_iota(jnp.int32, value.shape, 0) & 1 == 0
    return jnp.where(even, pltpu.roll(value, rows - 1, 0), pltpu.roll(value, 1, 0))


def kernel(sizes, qubits, couplings_at, fields_at, amp, done, held, mid, state, landed, back, low_c, low_s, high_c, high_s, cosine, sine, rows_w, lanes_w, couplings, fields, angle_sem, in_sem, own_sem, out_send, out_recv, near_send, near_recv, back_send, back_recv):
    parts, chunks, sub, _ = held.shape
    part_bits, chunk_bits = log2(parts), log2(chunks)
    lane_bits = log2(LANES)
    inner = lane_bits + log2(sub // 2)
    local_bits = inner + chunk_bits + part_bits
    far_first = qubits - part_bits
    chunk = parts * sub
    place = {axis: lax.axis_index(axis) for axis in AXES}
    me = place["gx"]
    near_at = place["gy"] * sizes["gz"] + place["gz"]

    stages = {axis: [] for axis in AXES}
    qubit = local_bits
    for axis in reversed(AXES):
        for bit in range(log2(sizes[axis])):
            stages[axis].append((axis, bit, qubit))
            qubit += 1
    near = stages["gy"] + list(reversed(stages["gz"]))
    plans = (near, near[1::-1] + near[2:])
    count = len(near)
    others = range(parts - 1)

    def partner(axis, bit):
        return tuple(place[a] ^ (1 << bit) if a == axis else place[a] for a in AXES)

    def other(n):
        return n + jnp.where(me <= n, 1, 0)

    def across(target):
        return tuple(target if a == "gx" else place[a] for a in AXES)

    def settle(ref, sem):
        pltpu.make_async_copy(ref, ref, sem).wait()

    loads = [pltpu.make_async_copy(amp.at[:, c], held.at[:, c], in_sem.at[min(c, 1)]) for c in range(chunks)]
    owns = [pltpu.make_async_copy(amp.at[me, c], mid.at[c, me], own_sem) for c in range(chunks)]
    barrier = pltpu.get_barrier_semaphore()
    for n in others:
        pl.semaphore_signal(barrier, inc=1, device_id=across(other(n)), device_id_type=MESH)
    for axis, bit, _ in near:
        pl.semaphore_signal(barrier, inc=1, device_id=partner(axis, bit), device_id_type=MESH)
    for load in loads:
        load.start()
    for own in owns:
        own.start()
    angles = [pltpu.make_async_copy(couplings_at, couplings, angle_sem.at[0]), pltpu.make_async_copy(fields_at, fields, angle_sem.at[1])]
    for angle in angles:
        angle.start()

    def out(c, n):
        target = other(n)
        return pltpu.make_async_remote_copy(
            src_ref=held.at[target, c],
            dst_ref=mid.at[c, me],
            send_sem=out_send,
            recv_sem=out_recv.at[c],
            device_id=across(target),
            device_id_type=MESH,
        )

    def send(c, k):
        axis, bit, _ = plans[c % 2][k]
        return pltpu.make_async_remote_copy(
            src_ref=state.at[k, c],
            dst_ref=landed.at[k, c],
            send_sem=near_send,
            recv_sem=near_recv.at[k, c],
            device_id=partner(axis, bit),
            device_id_type=MESH,
        )

    tail = sub // TAIL_PARTS
    late = chunks - 2
    groups = [(c, 1, 0, sub) for c in range(late)] + [(late, 2, t * tail, tail) for t in range(TAIL_PARTS)]
    arrivals = [0] * (late // 2) + [1] * (late - late // 2) + [2 + t for t in range(TAIL_PARTS)]

    def give(g, n):
        c, size, first, length = groups[g]
        span = pl.ds(first, length)
        target = other(n)
        return pltpu.make_async_remote_copy(
            src_ref=state.at[count, pl.ds(c, size), target, span],
            dst_ref=back.at[me, pl.ds(c, size), span],
            send_sem=back_send,
            recv_sem=back_recv.at[arrivals[g]],
            device_id=across(target),
            device_id_type=MESH,
        )

    pl.semaphore_wait(barrier, len(others) + count)
    for c in range(AHEAD):
        if c == 0:
            loads[c].wait()
        elif c == 1:
            settle(held.at[:, pl.ds(1, chunks - 1)], in_sem.at[1])
        for n in others:
            out(c, n).start()
    for angle in angles:
        angle.wait()

    for q in range(qubits):
        cosine[pl.ds(q, 1), :] = jnp.full((1, LANES), fields[q], jnp.float32)
    angles = cosine[...]
    cosine[...] = jnp.cos(angles)
    sine[...] = jnp.sin(angles)

    def angle_of(position, bonds):
        total = jnp.zeros(position.shape, jnp.float32)
        for q in bonds:
            parity = (position >> q ^ position >> ((q + 1) % qubits)) & 1
            total = total + couplings[q] * (1.0 - 2.0 * parity.astype(jnp.float32))
        return total

    quarter = math.pi / 2
    row = lax.broadcasted_iota(jnp.int32, (2 * sub, LANES), 0)
    lane = lax.broadcasted_iota(jnp.int32, (2 * sub, LANES), 1)
    top = jnp.where(row >= sub, 1, 0)
    position = (top << (qubits - 1)) + (((row - top * sub) >> 1) << lane_bits) + lane
    turns = bits_set(position, 0, inner) & 3
    low = angle_of(position, list(range(inner - 1)) + [qubits - 1]) + turns.astype(jnp.float32) * quarter
    low_c[...] = jnp.cos(low)
    low_s[...] = jnp.sin(low)
    number = lax.broadcasted_iota(jnp.int32, (2 * parts * chunks, LANES), 0)
    position = (
        ((number >> (1 + chunk_bits)) << far_first)
        + (near_at << local_bits)
        + (me << (inner + chunk_bits))
        + (((number >> 1) & (chunks - 1)) << inner)
        + ((number & 1) << (inner - 1))
    )
    turns = bits_set(position, inner, qubits) & 3
    high = angle_of(position, range(inner - 1, qubits - 1)) + turns.astype(jnp.float32) * quarter
    high_c[...] = jnp.cos(high)
    high_s[...] = jnp.sin(high)

    def matrix(shape, first_row, skip, mixed):
        there = lax.broadcasted_iota(jnp.int32, shape, 0) + first_row
        here = lax.broadcasted_iota(jnp.int32, shape, 1)
        total = jnp.ones(shape, jnp.float32)
        if skip:
            total = jnp.where((there ^ here) & ((1 << skip) - 1) == 0, total, 0.0)
        repeat = shape[1] // LANES
        for at, q in enumerate(mixed):
            bit = at + skip
            c_q = jnp.concatenate([cosine[pl.ds(q, 1), :]] * repeat, axis=1)
            s_q = jnp.concatenate([sine[pl.ds(q, 1), :]] * repeat, axis=1)
            up, left = there >> bit & 1, here >> bit & 1
            total = total * jnp.where(up ^ left == 1, s_q, jnp.where(up == 1, -c_q, c_q))
        return total

    lanes_w[...] = matrix((LANES, LANES), 0, 0, range(lane_bits))

    @pl.loop(0, chunk // 8)
    def _(step):
        at = pl.multiple_of(step * 8, 8)
        rows_w[pl.ds(at, 8), :] = matrix((8, chunk), at, 1, list(range(lane_bits, inner)) + list(range(far_first, qubits)))

    def turn(c):
        @pl.loop(0, sub // 8)
        def _(step):
            sign = jnp.where(lax.broadcasted_iota(jnp.int32, (8, LANES), 0) & 1 == 0, 1.0, -1.0)
            at = pl.multiple_of(step * 8, 8)
            half = step * 16 // sub
            for p in range(parts):
                c_low = low_c[pl.ds(pl.multiple_of(p * 2 // parts * sub + at, 8), 8), :]
                s_low = low_s[pl.ds(pl.multiple_of(p * 2 // parts * sub + at, 8), 8), :]
                which = (p * chunks + c) * 2 + half
                c_high = high_c[pl.ds(which, 1), :]
                s_high = high_s[pl.ds(which, 1), :]
                value = mid[c, p, pl.ds(at, 8), :]
                c_all = c_low * c_high - s_low * s_high
                s_all = s_low * c_high + c_low * s_high
                mid[c, p, pl.ds(at, 8), :] = value * c_all + swapped(value) * (s_all * sign)

    def local(c):
        for p in range(parts):
            mid[c, p] = jnp.dot(mid[c, p], lanes_w[...], precision=EXACT, preferred_element_type=jnp.float32)

        @pl.loop(0, parts)
        def _(p):
            at = pl.multiple_of(p * sub, sub)
            state[0, c, p] = jnp.dot(
                rows_w[pl.ds(at, sub), :], mid[c].reshape(chunk, LANES), precision=EXACT, preferred_element_type=jnp.float32
            )

    def combine(c, k):
        axis, bit, q = plans[c % 2][k]
        own = 1.0 - 2.0 * ((place[axis] >> bit) & 1).astype(jnp.float32)

        @pl.loop(0, sub // 16)
        def _(step):
            at = pl.multiple_of(step * 16, 16)
            c_q = cosine[pl.ds(q, 1), :] * own
            s_q = sine[pl.ds(q, 1), :]
            if k == count - 1:
                row = lax.broadcasted_iota(jnp.int32, (16, LANES), 0) + at
                lane = lax.broadcasted_iota(jnp.int32, (16, LANES), 1)
                inside = bits_set(((row >> 1) << lane_bits) + lane, 0, inner) + bits_set(near_at, 0, far_first - local_bits)
            for p in range(parts):
                value = c_q * state[k, c, p, pl.ds(at, 16), :] + s_q * landed[k, c, p, pl.ds(at, 16), :]
                if k == count - 1:
                    turns = inside + p.bit_count()
                    value = jnp.where(turns & 1 == 1, swapped(value), value)
                    value = jnp.where((turns + (row & 1)) & 2 == 2, -value, value)
                state[k + 1, c, p, pl.ds(at, 16), :] = value

    def keep(c):
        back[me, c] = state[count, c, me]

    events = [(c + (2 * k if k < count else 2 * k - 1.5), k, c) for c in range(chunks) for k in range(count + 1)]
    for _, k, c in sorted(events):
        if k == 0:
            if c == 0:
                settle(mid.at[:, 0], own_sem)
            settle(mid.at[c, pl.ds(0, parts - 1)], out_recv.at[c])
            if c + AHEAD < chunks:
                for n in others:
                    out(c + AHEAD, n).start()
            turn(c)
            local(c)
            send(c, 0).start()
        else:
            send(c, k - 1).wait_recv()
            combine(c, k - 1)
            if k < count:
                send(c, k).start()
            else:
                for n in others:
                    for g, group in enumerate(groups):
                        if group[0] + group[1] - 1 == c:
                            give(g, n).start()
                keep(c)

    settle(held.at[pl.ds(0, parts - 1)], out_send)
    settle(state.at[pl.ds(0, count)], near_send)

    def fold(values, bits, where):
        for bit in bits:
            c_q = cosine[pl.ds(inner + bit, 1), :]
            s_q = sine[pl.ds(inner + bit, 1), :]
            for n in where:
                if not n >> bit & 1:
                    one, two = values[n], values[n | 1 << bit]
                    values[n] = c_q * one + s_q * two
                    values[n | 1 << bit] = s_q * one - c_q * two

    part_span = range(chunk_bits, chunk_bits + part_bits)

    def early(first, length):
        where = [p * chunks + c for p in range(parts) for c in range(first, first + length)]
        inside = [bit for bit in range(chunk_bits) if length >> (bit + 1) and first % (2 << bit) == 0]

        @pl.loop(0, sub // 8)
        def _(step):
            at = pl.multiple_of(step * 8, 8)
            values = {n: back[n // chunks, n % chunks, pl.ds(at, 8), :] for n in where}
            fold(values, inside, where)
            fold(values, part_span, where)
            for n in where:
                back[n // chunks, n % chunks, pl.ds(at, 8), :] = values[n]

    def finish(first, size):
        @pl.loop(0, size // 8)
        def _(step):
            at = pl.multiple_of(first + step * 8, 8)
            sign = jnp.where(lax.broadcasted_iota(jnp.int32, (8, LANES), 0) & 1 == 0, 1.0, -1.0)
            values = [back[n // chunks, n % chunks, pl.ds(at, 8), :] for n in range(parts * chunks)]
            last = [n for n in range(parts * chunks) if n % chunks >= late]
            fold(values, part_span, last)
            fold(values, [0], last)
            for bit in range(1, chunk_bits):
                fold(values, [bit], [n for n in range(parts * chunks) if n % chunks >= chunks - (2 << bit)])
            for n, value in enumerate(values):
                turns = n.bit_count() & 3
                if turns & 1:
                    value = swapped(value) * (sign if turns == 1 else -sign)
                elif turns == 2:
                    value = -value
                done[n // chunks, n % chunks, pl.ds(at, 8), :] = value

    start = 0
    size = chunks // 2
    while start < late:
        if start == 0:
            settle(back.at[pl.ds(0, parts - 1), pl.ds(0, late // 2)], back_recv.at[0])
            settle(back.at[pl.ds(0, parts - 1), pl.ds(late // 2, late - late // 2)], back_recv.at[1])
        early(start, size)
        start += size
        size //= 2
    for t in range(TAIL_PARTS):
        settle(back.at[pl.ds(0, parts - 1), pl.ds(late, 2), pl.ds(t * tail, tail)], back_recv.at[2 + t])
        finish(t * tail, tail)
    settle(back.at[pl.ds(0, parts - 1)], back_send)


def solution(mesh):
    sizes = {axis: mesh.shape[axis] for axis in AXES}
    count = sum(log2(sizes[axis]) for axis in AXES[1:])

    def step(amplitudes, couplings, fields):
        local = amplitudes.shape[1]
        qubits = couplings.shape[0]
        rows = 2 * local // LANES
        parts = sizes[AXES[0]]
        chunks = 1 << CHUNK_BITS
        sub = rows // (parts * chunks)
        chunk = parts * sub
        table = -(-qubits // 8) * 8
        shape = (parts, chunks, sub, LANES)
        turned = (chunks, parts, sub, LANES)
        woven = amplitudes.reshape(2, local // LANES, LANES).transpose(1, 0, 2).reshape(shape)
        vmem = lambda *shape: pltpu.VMEM(shape, jnp.float32)
        dma = lambda *shape: pltpu.SemaphoreType.DMA(shape)
        result = pl.pallas_call(
            functools.partial(kernel, sizes, qubits),
            out_shape=pltpu.VMEM(shape, jnp.float32),
            in_specs=[pl.BlockSpec(memory_space=pltpu.HBM)] * 3,
            out_specs=pl.BlockSpec(memory_space=pltpu.VMEM),
            scratch_shapes=[
                vmem(*shape),
                vmem(*turned),
                vmem(count + 1, *turned),
                vmem(count, *turned),
                vmem(*shape),
                vmem(2 * sub, LANES),
                vmem(2 * sub, LANES),
                vmem(2 * parts * chunks, LANES),
                vmem(2 * parts * chunks, LANES),
                vmem(table, LANES),
                vmem(table, LANES),
                vmem(chunk, chunk),
                vmem(LANES, LANES),
                pltpu.SMEM((qubits,), jnp.float32),
                pltpu.SMEM((qubits,), jnp.float32),
                dma(2),
                dma(2),
                pltpu.SemaphoreType.DMA,
                pltpu.SemaphoreType.DMA,
                dma(chunks),
                pltpu.SemaphoreType.DMA,
                dma(count, chunks),
                pltpu.SemaphoreType.DMA,
                dma(2 + TAIL_PARTS),
            ],
            compiler_params=pltpu.CompilerParams(
                collective_id=0, has_side_effects=True, vmem_limit_bytes=VMEM - 4 * rows * LANES
            ),
        )(couplings, fields, woven)
        return result.reshape(local // LANES, 2, LANES).transpose(1, 0, 2).reshape(2, local)

    placed = (P(None, AXES), P(), P())
    return jax.shard_map(step, mesh=mesh, in_specs=placed, out_specs=P(None, AXES), check_vma=False)
```

time: 101 us -> 95.6 us (0.947); the launches traced: 99.5 us -> 95.3 us
  Pallas kernels: 98.1 us -> 94 us
    pallas_call x1, Pallas kernels: 98.1 us -> 94 us  [step(): pl.pallas_call(functools.partial(kernel, sizes, qubits), out_shape=pltpu....]
where the time goes in v1:
time: 95.6 us; the launch traced here: 95.3 us
  Pallas kernels  94 us (98%)
  local copies, waits for them, and re-layouts  1.32 us (1%)
    pallas_call x1, Pallas kernels, step(): pl.pallas_call(functools.partial(kernel, sizes, qubits), out_shape=pltpu....  94 us

profile of v1, /device:TPU:9, one launch (start us, length us, event | category | flops | bytes accessed | tf_op | source)
XLA Modules:
  0.0 95.3 jit_solution(3260412467037733237)
XLA Ops:
  0.0 94.0 %shard_map.37 = f32[4,8,128,128]{3,2,1,0:T(8,128)S(1)} custom-call(f32[23]{0:T(128)} %couplings_at.1, f32[23]{0:T(128)} %fields_at.1, f32[4,8,128,128]{3,2,1,0:T(8,128)} %bitcast.11), custom_call_target="tpu_custom_call" | custom-call | tf_op jit(solution)/shard_map/pallas_call | solution.py:352
  94.0 1.3 %copy.7 = f32[2,262144]{1,0:T(2,128)} copy(f32[2,262144]{1,0:T(2,128)S(1)} %bitcast.10) | data formatting | bytes 4194304

commit v2 on v1

--- a/solution.py
+++ b/solution.py
@@ -13,7 +13,8 @@
 LANES = 128
 CHUNK_BITS = 3
 TAIL_PARTS = 8
-AHEAD = 3
+AHEAD = 4
+STEP = 1.6
 VMEM = 67043328
 EXACT = lax.Precision.HIGHEST
 
@@ -35,7 +36,7 @@
     return jnp.where(even, pltpu.roll(value, rows - 1, 0), pltpu.roll(value, 1, 0))
 
 
-def kernel(sizes, qubits, couplings_at, fields_at, amp, done, held, mid, state, landed, back, low_c, low_s, high_c, high_s, cosine, sine, rows_w, lanes_w, couplings, fields, angle_sem, in_sem, own_sem, out_send, out_recv, near_send, near_recv, back_send, back_recv):
+def kernel(sizes, qubits, couplings_at, fields_at, amp, done, held, mid, state, landed, final, back, low_c, low_s, high_c, high_s, cosine, sine, rows_w, lanes_w, couplings, fields, far_ready, near_ready, angle_sem, in_sem, own_sem, out_send, out_recv, near_send, near_recv, back_send, back_recv):
     parts, chunks, sub, _ = held.shape
     part_bits, chunk_bits = log2(parts), log2(chunks)
     lane_bits = log2(LANES)
@@ -57,12 +58,16 @@
     plans = (near, near[1::-1] + near[2:])
     count = len(near)
     others = range(parts - 1)
+    late = chunks - 2
 
     def partner(axis, bit):
         return tuple(place[a] ^ (1 << bit) if a == axis else place[a] for a in AXES)
 
-    def other(n):
-        return n + jnp.where(me <= n, 1, 0)
+    def other(n, mirrored=True):
+        mirror = me < parts // 2
+        seen = jnp.where(mirror, parts - 1 - me, me) if mirrored else me
+        target = n + jnp.where(seen <= n, 1, 0)
+        return jnp.where(mirror, parts - 1 - target, target) if mirrored else target
 
     def across(target):
         return tuple(target if a == "gx" else place[a] for a in AXES)
@@ -71,12 +76,22 @@
         pltpu.make_async_copy(ref, ref, sem).wait()
 
     loads = [pltpu.make_async_copy(amp.at[:, c], held.at[:, c], in_sem.at[min(c, 1)]) for c in range(chunks)]
-    owns = [pltpu.make_async_copy(amp.at[me, c], mid.at[c, me], own_sem) for c in range(chunks)]
+    owns = [pltpu.make_async_copy(amp.at[me, c], mid.at[c, me], own_sem) for c in range(late)]
     barrier = pltpu.get_barrier_semaphore()
     for n in others:
-        pl.semaphore_signal(barrier, inc=1, device_id=across(other(n)), device_id_type=MESH)
-    for axis, bit, _ in near:
-        pl.semaphore_signal(barrier, inc=1, device_id=partner(axis, bit), device_id_type=MESH)
+        target = other(n)
+
+        @pl.when(jnp.logical_or(target > me, target < parts // 2))
+        def _():
+            pl.semaphore_signal(barrier, inc=1, device_id=across(target), device_id_type=MESH)
+
+    below = [place[axis] >> bit & 1 for axis, bit, _ in near]
+    for down, (axis, bit, _) in zip(below, near):
+
+        @pl.when(down == 0)
+        def _():
+            pl.semaphore_signal(barrier, inc=1, device_id=partner(axis, bit), device_id_type=MESH)
+
     for load in loads:
         load.start()
     for own in owns:
@@ -84,11 +99,18 @@
     angles = [pltpu.make_async_copy(couplings_at, couplings, angle_sem.at[0]), pltpu.make_async_copy(fields_at, fields, angle_sem.at[1])]
     for angle in angles:
         angle.start()
+    pl.semaphore_wait(barrier, sum(below) + jnp.where(me < parts // 2, parts - 1, me))
+    for n in others:
+        target = other(n)
+
+        @pl.when(jnp.logical_and(target < me, target >= parts // 2))
+        def _():
+            pl.semaphore_signal(far_ready.at[me], inc=1, device_id=across(target), device_id_type=MESH)
 
     def out(c, n):
         target = other(n)
         return pltpu.make_async_remote_copy(
-            src_ref=held.at[target, c],
+            src_ref=held.at[target, c] if c < late else state.at[count, c, target],
             dst_ref=mid.at[c, me],
             send_sem=out_send,
             recv_sem=out_recv.at[c],
@@ -102,22 +124,22 @@
             src_ref=state.at[k, c],
             dst_ref=landed.at[k, c],
             send_sem=near_send,
-            recv_sem=near_recv.at[k, c],
+            recv_sem=near_recv.at[k, c // 2],
             device_id=partner(axis, bit),
             device_id_type=MESH,
         )
 
     tail = sub // TAIL_PARTS
-    late = chunks - 2
     groups = [(c, 1, 0, sub) for c in range(late)] + [(late, 2, t * tail, tail) for t in range(TAIL_PARTS)]
-    arrivals = [0] * (late // 2) + [1] * (late - late // 2) + [2 + t for t in range(TAIL_PARTS)]
+    pairs = late // 2
+    arrivals = [c // 2 for c in range(late)] + [pairs + t for t in range(TAIL_PARTS)]
 
     def give(g, n):
         c, size, first, length = groups[g]
         span = pl.ds(first, length)
-        target = other(n)
+        target = other(n, c < late)
         return pltpu.make_async_remote_copy(
-            src_ref=state.at[count, pl.ds(c, size), target, span],
+            src_ref=state.at[count, pl.ds(c, size), target, span] if c < late else final.at[:, target, span],
             dst_ref=back.at[me, pl.ds(c, size), span],
             send_sem=back_send,
             recv_sem=back_recv.at[arrivals[g]],
@@ -125,14 +147,30 @@
             device_id_type=MESH,
         )
 
-    pl.semaphore_wait(barrier, len(others) + count)
-    for c in range(AHEAD):
-        if c == 0:
-            loads[c].wait()
-        elif c == 1:
-            settle(held.at[:, pl.ds(1, chunks - 1)], in_sem.at[1])
-        for n in others:
-            out(c, n).start()
+    def first(low):
+        for c in range(AHEAD):
+            if low and c == 0:
+                loads[c].wait()
+            elif low and c == 1:
+                settle(held.at[:, pl.ds(1, chunks - 1)], in_sem.at[1])
+            for n in others:
+                target = other(n)
+
+                known = jnp.logical_or(target < me, me < parts // 2)
+
+                @pl.when(known if low else jnp.logical_not(known))
+                def _():
+                    if not low and c == 0:
+                        pl.semaphore_wait(far_ready.at[target], 1)
+                    out(c, n).start()
+
+    first(True)
+    for down, (axis, bit, _) in zip(below, near):
+
+        @pl.when(down == 1)
+        def _():
+            pl.semaphore_signal(near_ready, inc=1, device_id=partner(axis, bit), device_id_type=MESH)
+
     for angle in angles:
         angle.wait()
 
@@ -158,18 +196,48 @@
     low = angle_of(position, list(range(inner - 1)) + [qubits - 1]) + turns.astype(jnp.float32) * quarter
     low_c[...] = jnp.cos(low)
     low_s[...] = jnp.sin(low)
-    number = lax.broadcasted_iota(jnp.int32, (2 * parts * chunks, LANES), 0)
+    table = 2 * parts * chunks
+    number = lax.broadcasted_iota(jnp.int32, high_c.shape, 0)
+    rest = number - table
+    before = rest >= 0
     position = (
-        ((number >> (1 + chunk_bits)) << far_first)
+        (jnp.where(before, me, number >> (1 + chunk_bits)) << far_first)
         + (near_at << local_bits)
-        + (me << (inner + chunk_bits))
-        + (((number >> 1) & (chunks - 1)) << inner)
+        + (jnp.where(before, rest >> 2, me) << (inner + chunk_bits))
+        + (jnp.where(before, late + (rest >> 1 & 1), (number >> 1) & (chunks - 1)) << inner)
         + ((number & 1) << (inner - 1))
     )
     turns = bits_set(position, inner, qubits) & 3
     high = angle_of(position, range(inner - 1, qubits - 1)) + turns.astype(jnp.float32) * quarter
     high_c[...] = jnp.cos(high)
     high_s[...] = jnp.sin(high)
+    first(False)
+
+    def turned(value, low_at, high_at):
+        sign = jnp.where(lax.broadcasted_iota(jnp.int32, (8, LANES), 0) & 1 == 0, 1.0, -1.0)
+        c_low = low_c[pl.ds(pl.multiple_of(low_at, 8), 8), :]
+        s_low = low_s[pl.ds(pl.multiple_of(low_at, 8), 8), :]
+        c_high = high_c[pl.ds(high_at, 1), :]
+        s_high = high_s[pl.ds(high_at, 1), :]
+        c_all = c_low * c_high - s_low * s_high
+        s_all = s_low * c_high + c_low * s_high
+        return value * c_all + swapped(value) * (s_all * sign)
+
+    @pl.loop(0, sub // 8)
+    def _(step):
+        at = pl.multiple_of(step * 8, 8)
+        half = step * 16 // sub
+        for c in (late, late + 1):
+            for p in range(parts):
+                high_at = table + p * 4 + (c - late) * 2 + half
+                state[0, c, p, pl.ds(at, 8), :] = turned(held[p, c, pl.ds(at, 8), :], me * 2 // parts * sub + at, high_at)
+
+    @pl.when(sum(below) < count)
+    def _():
+        pl.semaphore_wait(near_ready, count - sum(below))
+
+    for c in (late, late + 1):
+        send(c, 0).start()
 
     def matrix(shape, first_row, skip, mixed):
         there = lax.broadcasted_iota(jnp.int32, shape, 0) + first_row
@@ -196,30 +264,34 @@
     def turn(c):
         @pl.loop(0, sub // 8)
         def _(step):
-            sign = jnp.where(lax.broadcasted_iota(jnp.int32, (8, LANES), 0) & 1 == 0, 1.0, -1.0)
             at = pl.multiple_of(step * 8, 8)
             half = step * 16 // sub
             for p in range(parts):
-                c_low = low_c[pl.ds(pl.multiple_of(p * 2 // parts * sub + at, 8), 8), :]
-                s_low = low_s[pl.ds(pl.multiple_of(p * 2 // parts * sub + at, 8), 8), :]
-                which = (p * chunks + c) * 2 + half
-                c_high = high_c[pl.ds(which, 1), :]
-                s_high = high_s[pl.ds(which, 1), :]
-                value = mid[c, p, pl.ds(at, 8), :]
-                c_all = c_low * c_high - s_low * s_high
-                s_all = s_low * c_high + c_low * s_high
-                mid[c, p, pl.ds(at, 8), :] = value * c_all + swapped(value) * (s_all * sign)
-
-    def local(c):
+                mid[c, p, pl.ds(at, 8), :] = turned(mid[c, p, pl.ds(at, 8), :], p * 2 // parts * sub + at, (p * chunks + c) * 2 + half)
+
+    def local(c, target):
         for p in range(parts):
             mid[c, p] = jnp.dot(mid[c, p], lanes_w[...], precision=EXACT, preferred_element_type=jnp.float32)
 
         @pl.loop(0, parts)
         def _(p):
             at = pl.multiple_of(p * sub, sub)
-            state[0, c, p] = jnp.dot(
+            target[p] = jnp.dot(
                 rows_w[pl.ds(at, sub), :], mid[c].reshape(chunk, LANES), precision=EXACT, preferred_element_type=jnp.float32
             )
+
+    def each_part(step, source, target, straight):
+        at = pl.multiple_of(step * 16, 16)
+        row = lax.broadcasted_iota(jnp.int32, (16, LANES), 0) + at
+        lane = lax.broadcasted_iota(jnp.int32, (16, LANES), 1)
+        inside = bits_set(((row >> 1) << lane_bits) + lane, 0, inner) + bits_set(near_at, 0, far_first - local_bits)
+        for p in range(parts):
+            value = source(p, at)
+            if straight:
+                turns = inside + p.bit_count()
+                value = jnp.where(turns & 1 == 1, swapped(value), value)
+                value = jnp.where((turns + (row & 1)) & 2 == 2, -value, value)
+            target[p, pl.ds(at, 16), :] = value
 
     def combine(c, k):
         axis, bit, q = plans[c % 2][k]
@@ -227,49 +299,57 @@
 
         @pl.loop(0, sub // 16)
         def _(step):
-            at = pl.multiple_of(step * 16, 16)
             c_q = cosine[pl.ds(q, 1), :] * own
             s_q = sine[pl.ds(q, 1), :]
-            if k == count - 1:
-                row = lax.broadcasted_iota(jnp.int32, (16, LANES), 0) + at
-                lane = lax.broadcasted_iota(jnp.int32, (16, LANES), 1)
-                inside = bits_set(((row >> 1) << lane_bits) + lane, 0, inner) + bits_set(near_at, 0, far_first - local_bits)
-            for p in range(parts):
-                value = c_q * state[k, c, p, pl.ds(at, 16), :] + s_q * landed[k, c, p, pl.ds(at, 16), :]
-                if k == count - 1:
-                    turns = inside + p.bit_count()
-                    value = jnp.where(turns & 1 == 1, swapped(value), value)
-                    value = jnp.where((turns + (row & 1)) & 2 == 2, -value, value)
-                state[k + 1, c, p, pl.ds(at, 16), :] = value
-
-    def keep(c):
-        back[me, c] = state[count, c, me]
-
-    events = [(c + (2 * k if k < count else 2 * k - 1.5), k, c) for c in range(chunks) for k in range(count + 1)]
-    for _, k, c in sorted(events):
-        if k == 0:
+            source = lambda p, at: c_q * state[k, c, p, pl.ds(at, 16), :] + s_q * landed[k, c, p, pl.ds(at, 16), :]
+            each_part(step, source, state.at[k + 1, c], k == count - 1 and c < late)
+
+    def straighten(ref):
+        @pl.loop(0, sub // 16)
+        def _(step):
+            each_part(step, lambda p, at: ref[p, pl.ds(at, 16), :], ref, True)
+
+    def return_all(c):
+        sends = [(g, n) for n in others for g, group in enumerate(groups) if group[0] + group[1] - 1 == c]
+        for g, n in sends:
+            give(g, n).start()
+
+    ARRIVE, MEET, LEAVE = range(3)
+    events = [(c, ARRIVE, c, 0) for c in range(chunks)]
+    for c in range(1, late, 2):
+        events += [(c + STEP * min(k, count - 1) + k // count * 0.2, MEET, c, k) for k in range(1, count + 1)]
+    events += [(min(k, count - 1) - 1.5 + k // count * 0.1, MEET, chunks - 1, k) for k in range(1, count + 1)]
+    events.append((4 * chunks, LEAVE, chunks - 1, 0))
+    for _, what, c, k in sorted(events):
+        if what == ARRIVE:
             if c == 0:
-                settle(mid.at[:, 0], own_sem)
+                settle(mid.at[pl.ds(0, late), 0], own_sem)
             settle(mid.at[c, pl.ds(0, parts - 1)], out_recv.at[c])
             if c + AHEAD < chunks:
                 for n in others:
                     out(c + AHEAD, n).start()
-            turn(c)
-            local(c)
-            send(c, 0).start()
+            if c < late:
+                turn(c)
+                local(c, state.at[0, c])
+                send(c, 0).start()
+            else:
+                mid[c, me] = state[count, c, me]
+                local(c, final.at[c - late])
+                straighten(final.at[c - late])
+                back[me, c] = final[c - late, me]
+        elif what == MEET:
+            settle(landed.at[k - 1, pl.ds(c - 1, 2)], near_recv.at[k - 1, c // 2])
+            for each in (c - 1, c):
+                combine(each, k - 1)
+                if k < count:
+                    send(each, k).start()
+                elif c < late:
+                    back[me, each] = state[count, each, me]
+                    return_all(each)
         else:
-            send(c, k - 1).wait_recv()
-            combine(c, k - 1)
-            if k < count:
-                send(c, k).start()
-            else:
-                for n in others:
-                    for g, group in enumerate(groups):
-                        if group[0] + group[1] - 1 == c:
-                            give(g, n).start()
-                keep(c)
-
-    settle(held.at[pl.ds(0, parts - 1)], out_send)
+            return_all(c)
+
+    settle(mid.at[:, pl.ds(0, parts - 1)], out_send)
     settle(state.at[pl.ds(0, count)], near_send)
 
     def fold(values, bits, where):
@@ -316,17 +396,14 @@
                     value = -value
                 done[n // chunks, n % chunks, pl.ds(at, 8), :] = value
 
-    start = 0
-    size = chunks // 2
-    while start < late:
-        if start == 0:
-            settle(back.at[pl.ds(0, parts - 1), pl.ds(0, late // 2)], back_recv.at[0])
-            settle(back.at[pl.ds(0, parts - 1), pl.ds(late // 2, late - late // 2)], back_recv.at[1])
-        early(start, size)
-        start += size
-        size //= 2
+    start, size = 0, chunks // 2
+    for pair in range(pairs):
+        settle(back.at[pl.ds(0, parts - 1), pl.ds(2 * pair, 2)], back_recv.at[pair])
+        if start + size == 2 * pair + 2:
+            early(start, size)
+            start, size = start + size, size // 2
     for t in range(TAIL_PARTS):
-        settle(back.at[pl.ds(0, parts - 1), pl.ds(late, 2), pl.ds(t * tail, tail)], back_recv.at[2 + t])
+        settle(back.at[pl.ds(0, parts - 1), pl.ds(late, 2), pl.ds(t * tail, tail)], back_recv.at[pairs + t])
         finish(t * tail, tail)
     settle(back.at[pl.ds(0, parts - 1)], back_send)
 
@@ -359,26 +436,29 @@
                 vmem(*turned),
                 vmem(count + 1, *turned),
                 vmem(count, *turned),
+                vmem(2, *turned[1:]),
                 vmem(*shape),
                 vmem(2 * sub, LANES),
                 vmem(2 * sub, LANES),
-                vmem(2 * parts * chunks, LANES),
-                vmem(2 * parts * chunks, LANES),
+                vmem(2 * parts * (chunks + 2), LANES),
+                vmem(2 * parts * (chunks + 2), LANES),
                 vmem(table, LANES),
                 vmem(table, LANES),
                 vmem(chunk, chunk),
                 vmem(LANES, LANES),
                 pltpu.SMEM((qubits,), jnp.float32),
                 pltpu.SMEM((qubits,), jnp.float32),
+                pltpu.SemaphoreType.REGULAR((parts,)),
+                pltpu.SemaphoreType.REGULAR,
                 dma(2),
                 dma(2),
                 pltpu.SemaphoreType.DMA,
                 pltpu.SemaphoreType.DMA,
                 dma(chunks),
                 pltpu.SemaphoreType.DMA,
-                dma(count, chunks),
+                dma(count, chunks // 2),
                 pltpu.SemaphoreType.DMA,
-                dma(2 + TAIL_PARTS),
+                dma(chunks // 2 - 1 + TAIL_PARTS),
             ],
             compiler_params=pltpu.CompilerParams(
                 collective_id=0, has_side_effects=True, vmem_limit_bytes=VMEM - 4 * rows * LANES

time: 95.6 us -> 95.2 us (level)
  no operation moved by 1% of the time
where the time goes in v2:
time: 95.2 us; the launch traced here: 95 us
  Pallas kernels  93.7 us (98%)
  local copies, waits for them, and re-layouts  1.32 us (1%)
    pallas_call x1, Pallas kernels, step(): pl.pallas_call(functools.partial(kernel, sizes, qubits), out_shape=pltpu....  93.7 us

profile of v2, /device:TPU:9, one launch (start us, length us, event | category | flops | bytes accessed | tf_op | source)
XLA Modules:
  0.0 95.0 jit_solution(15787971781382350591)
XLA Ops:
  0.0 93.7 %shard_map.37 = f32[4,8,128,128]{3,2,1,0:T(8,128)S(1)} custom-call(f32[23]{0:T(128)} %couplings_at.1, f32[23]{0:T(128)} %fields_at.1, f32[4,8,128,128]{3,2,1,0:T(8,128)} %bitcast.11), custom_call_target="tpu_custom_call" | custom-call | tf_op jit(solution)/shard_map/pallas_call | solution.py:429
  93.7 1.3 %copy.7 = f32[2,262144]{1,0:T(2,128)} copy(f32[2,262144]{1,0:T(2,128)S(1)} %bitcast.10) | data formatting | bytes 4194304

commit v3 on v2

--- a/solution.py
+++ b/solution.py
@@ -105,7 +105,7 @@
 
         @pl.when(jnp.logical_and(target < me, target >= parts // 2))
         def _():
-            pl.semaphore_signal(far_ready.at[me], inc=1, device_id=across(target), device_id_type=MESH)
+            pl.semaphore_signal(far_ready.at[me - parts // 2], inc=1, device_id=across(target), device_id_type=MESH)
 
     def out(c, n):
         target = other(n)
@@ -137,7 +137,7 @@
     def give(g, n):
         c, size, first, length = groups[g]
         span = pl.ds(first, length)
-        target = other(n, c < late)
+        target = other(n, c < late - 2)
         return pltpu.make_async_remote_copy(
             src_ref=state.at[count, pl.ds(c, size), target, span] if c < late else final.at[:, target, span],
             dst_ref=back.at[me, pl.ds(c, size), span],
@@ -161,7 +161,7 @@
                 @pl.when(known if low else jnp.logical_not(known))
                 def _():
                     if not low and c == 0:
-                        pl.semaphore_wait(far_ready.at[target], 1)
+                        pl.semaphore_wait(far_ready.at[target - parts // 2], 1)
                     out(c, n).start()
 
     first(True)
@@ -448,7 +448,7 @@
                 vmem(LANES, LANES),
                 pltpu.SMEM((qubits,), jnp.float32),
                 pltpu.SMEM((qubits,), jnp.float32),
-                pltpu.SemaphoreType.REGULAR((parts,)),
+                pltpu.SemaphoreType.REGULAR((parts // 2,)),
                 pltpu.SemaphoreType.REGULAR,
                 dma(2),
                 dma(2),

time: 95.2 us -> 95.2 us (level)
  no operation moved by 1% of the time
where the time goes in v3:
time: 95.2 us; the launch traced here: 95 us
  Pallas kernels  93.7 us (98%)
  local copies, waits for them, and re-layouts  1.32 us (1%)
    pallas_call x1, Pallas kernels, step(): pl.pallas_call(functools.partial(kernel, sizes, qubits), out_shape=pltpu....  93.7 us

profile of v3, /device:TPU:9, one launch (start us, length us, event | category | flops | bytes accessed | tf_op | source)
XLA Modules:
  0.0 95.0 jit_solution(847638849587318158)
XLA Ops:
  0.0 93.7 %shard_map.37 = f32[4,8,128,128]{3,2,1,0:T(8,128)S(1)} custom-call(f32[23]{0:T(128)} %couplings_at.1, f32[23]{0:T(128)} %fields_at.1, f32[4,8,128,128]{3,2,1,0:T(8,128)} %bitcast.11), custom_call_target="tpu_custom_call" | custom-call | tf_op jit(solution)/shard_map/pallas_call | solution.py:429
  93.7 1.3 %copy.7 = f32[2,262144]{1,0:T(2,128)} copy(f32[2,262144]{1,0:T(2,128)S(1)} %bitcast.10) | data formatting | bytes 4194304
